TPU v7x, 32 devices: a whole 2x2x4 slice. The times are simulated.
32 devices in a mesh: member: 8 (over y, x, core), domain: 4 (over z).
Axes of the slice: x: 2, y: 2, z: 4, core: 2. Of those that a mesh axis runs over, the one named last changes fastest.
Arguments:
- ensemble: bfloat16 [256, 2, 16, 512], P('member', None, None, 'domain'), may hold values from -4 to 4
- obs_value: float32 [8, 1024], P('member', 'domain'), may hold values from -6 to 6
- obs_prec: float32 [8, 1024], P('member', 'domain'), may hold values from 1 to 10
- obs_row: int32 [8, 1024], P('member', 'domain'), may hold values from 0 to 1
- obs_col: int32 [8, 1024], P('member', 'domain'), may hold values from 0 to 127
- loc_mask: int32 [8, 16], P('member', 'domain'), may hold values 0 or 1
Outputs:
- analysis: bfloat16 [256, 2, 16, 512], P('member', None, None, 'domain')
All inputs are finite; a program needn't handle non-finite values. No bound on the sum of `loc_mask` on one device may be relied on, other than what follows from the above.
Results may differ from a plain program's by a relative error of at most 0.0075.
Values may be sent and summed in bfloat16 or wider, within the bound.
A program may use at most 64 MiB of HBM per device.

v0:
```python
import jax
import jax.numpy as jnp
from jax import lax
from jax.sharding import PartitionSpec as P

ADVECT = 0.4
DIFFUSE = 0.15
OBS_WIND = 0.5


def padded(cells, sides, width):
    for axis, dim in sides:
        count = lax.axis_size(axis)
        head = lax.slice_in_dim(cells, 0, width, axis=dim)
        tail = lax.slice_in_dim(cells, cells.shape[dim] - width, cells.shape[dim], axis=dim)
        cells = jnp.concatenate(
            [
                lax.ppermute(tail, axis, [(i, (i + 1) % count) for i in range(count)]),
                cells,
                lax.ppermute(head, axis, [((i + 1) % count, i) for i in range(count)]),
            ],
            axis=dim,
        )
    return cells


def step_forward(central_cell, east_cells, west_cells, north_cells, south_cells):
    middle = central_cell.astype(jnp.float32)
    east_side = east_cells.astype(jnp.float32)
    west_side = west_cells.astype(jnp.float32)
    laplace = (
        east_side
        + west_side
        + north_cells.astype(jnp.float32)
        + south_cells.astype(jnp.float32)
        - 4.0 * middle
    )
    wind_field = middle[:, 0:1]
    return (
        middle - ADVECT * 0.5 * wind_field * (east_side - west_side) + DIFFUSE * laplace
    ).astype(jnp.bfloat16)


def observe(local_region, obs_index, observed, precision):
    member_states = local_region.shape[0]
    wind_field = local_region[:, 0].reshape(member_states, -1)
    tracer = local_region[:, 1].reshape(member_states, -1)
    equivalent = jnp.take(tracer, obs_index, axis=1).astype(jnp.float32) + OBS_WIND * jnp.take(
        wind_field, obs_index, axis=1
    ).astype(jnp.float32)
    central_cell = jnp.mean(equivalent, axis=0)
    scaled = (equivalent - central_cell) * (member_states - 1) ** (-0.5)
    return jnp.concatenate(
        [scaled, (observed - central_cell)[None], precision[None]], axis=0
    ).astype(jnp.bfloat16)


def block_weights(local_rows, block_mask, parts):
    member_states = local_rows.shape[0] - 2
    tapering = jnp.array([0.5, 1.0, 1.0, 0.5], jnp.float32) * block_mask.astype(jnp.float32)
    block_cols = local_rows.shape[1] // len(parts)
    factor = jnp.repeat(tapering[jnp.array(parts)], block_cols)
    return local_rows[member_states + 1].astype(jnp.float32) * factor


def contributions(local_rows, weight):
    member_states = local_rows.shape[0] - 2
    anomaly_obs = local_rows[:member_states]
    innovation = local_rows[member_states].astype(jnp.float32)
    weighted = (anomaly_obs.astype(jnp.float32) * weight).astype(jnp.bfloat16)
    cross_term = lax.dot_general(
        weighted, anomaly_obs, (((1,), (1,)), ((), ())), preferred_element_type=jnp.float32
    )
    forcing = jnp.dot(weighted.astype(jnp.float32), innovation, precision=lax.Precision.HIGHEST)
    return (cross_term, forcing)


def analyse(local_region, cross_term, forcing):
    member_states = local_region.shape[0]
    cells = local_region.reshape(member_states, -1)
    ens_mean = jnp.mean(cells.astype(jnp.float32), axis=0)
    anomalies = (cells.astype(jnp.float32) - ens_mean).astype(jnp.bfloat16)
    identity = jnp.eye(member_states, dtype=jnp.float32)
    cross_half = cross_term.astype(jnp.bfloat16)
    squared = jnp.dot(cross_half, cross_half, preferred_element_type=jnp.float32)
    row_bound = jnp.sqrt(jnp.max(jnp.sum(jnp.abs(squared), axis=1)))
    half_width = (row_bound + 1.0) / 2.0
    theta = 1.0 + half_width
    ratio_sigma = theta / half_width
    rho_first = 1.0 / ratio_sigma
    first_resid = (1.0 - 1.0 / theta) * identity - cross_term / theta
    first_step = first_resid / theta
    applied = first_step + ((theta - 1.0) * cross_term - squared) / (theta * theta)
    second_resid = first_resid - applied
    rho_second = 1.0 / (2.0 * ratio_sigma - rho_first)
    second_step = rho_second * rho_first * first_step + 2.0 * rho_second / half_width * second_resid
    inverse = identity / theta + first_step + second_step
    mean_weights = jnp.dot(inverse, forcing, precision=lax.Precision.HIGHEST)
    transform = (
        0.5 * (identity + inverse) + mean_weights[:, None] * (member_states - 1) ** (-0.5)
    ).astype(jnp.bfloat16)
    increment = lax.dot_general(
        transform, anomalies, (((0,), (0,)), ((), ())), preferred_element_type=jnp.float32
    )
    return (ens_mean + increment).astype(jnp.bfloat16).reshape(local_region.shape)


def on_device(ensemble, obs_value, obs_prec, obs_row, obs_col, loc_mask):
    padded_region = padded(ensemble, (("domain", 3),), 1)
    central_cell = padded_region[..., 1:-1]
    predicted_state = step_forward(
        central_cell,
        padded_region[..., 2:],
        padded_region[..., :-2],
        jnp.roll(central_cell, -1, axis=2),
        jnp.roll(central_cell, 1, axis=2),
    )
    local_region = lax.all_to_all(
        predicted_state, "member", split_axis=2, concat_axis=0, tiled=True
    )
    obs_index = obs_row[0] * local_region.shape[3] + obs_col[0]
    stacked = observe(local_region, obs_index, obs_value[0], obs_prec[0])
    half_cols = stacked.shape[1] // 2
    local_rows = padded(stacked, (("domain", 1),), half_cols)
    weight = block_weights(local_rows, loc_mask[0], [0, 1, 2, 3])
    cross_term, forcing = contributions(local_rows, weight)
    analysis = analyse(local_region, cross_term, forcing)
    return lax.all_to_all(analysis, "member", split_axis=0, concat_axis=2, tiled=True)


def solution(mesh):
    in_specs = (
        P("member", None, None, "domain"),
        P("member", "domain"),
        P("member", "domain"),
        P("member", "domain"),
        P("member", "domain"),
        P("member", "domain"),
    )
    out_specs = P("member", None, None, "domain")
    return jax.shard_map(
        on_device, mesh=mesh, in_specs=in_specs, out_specs=out_specs, check_vma=False
    )
```

profile of v0, /device:TPU:0, one launch (start us, length us, event | category | flops | bytes accessed | tf_op | source)
XLA Modules:
  0.0 49.0 jit_solution(11393552374662665479)
XLA Ops:
  0.0 1.2 %fusion.37 = (bf16[32,2,16,1]{3,2,1,0:T(8,128)(2,1)S(1)}, bf16[32,2,16,1]{3,2,1,0:T(8,128)(2,1)S(1)}) fusion(bf16[32,2,16,128]{3,2,1,0:T(8,128)(2,1)} %param.10), kind=kLoop, calls=%fused_computation.75 | loop fusion | bytes 8192 | tf_op jit(solution)/shard_map/slice | solution.py:14
  1.2 0.4 copy.71
  1.6 5.1 %collective-permute-start = (bf16[32,2,16,1]{0,2,3,1:T(8,128)(2,1)S(1)}, bf16[32,2,16,1]{0,2,3,1:T(8,128)(2,1)S(1)}, u32[]{:S(2)}, u32[]{:S(2)}) collective-permute-start(bf16[32,2,16,1]{0,2,3,1:T(8,128)(2,1)S(1)} %copy.71), channel_id=1, source_target_pairs={{1,0},{2,1},{3,2},{0,3},{5,4},{6,5},{7,6},{4,7},{9,8},{10,9},{11,1... | collective-permute-start | bytes 6152 | tf_op jit(solution)/shard_map/ppermute | solution.py:20
  6.7 0.4 copy.72
  7.5 0.6 %copy-done.1 = s32[1,256]{1,0:T(1,128)S(1)} copy-done((s32[1,256]{1,0:T(1,128)S(1)}, s32[1,256]{1,0:T(1,128)}, u32[]{:S(2)}) %copy-start.1) | copy-done | bytes 1048
  8.1 0.6 %copy-done.5 = s32[1,4]{1,0:T(1,128)S(1)} copy-done((s32[1,4]{1,0:T(1,128)S(1)}, s32[1,4]{1,0:T(1,128)}, u32[]{:S(2)}) %copy-start.5) | copy-done | bytes 40
  8.8 0.2 pad_maximum_fusion.3
  9.0 0.3 copy.58
  9.3 3.2 %collective-permute-done.1 = bf16[32,2,16,1]{0,2,3,1:T(8,128)(2,1)S(1)} collective-permute-done((bf16[32,2,16,1]{0,2,3,1:T(8,128)(2,1)S(1)}, bf16[32,2,16,1]{0,2,3,1:T(8,128)(2,1)S(1)}, u32[]{:S(2)}, u32[]{:S(2)}) %collective-permute-start.1) | collective-permute-done | bytes 2080 | tf_op jit(solution)/shard_map/ppermute | solution.py:18
  12.5 0.3 copy.60
  12.8 1.2 %fusion.4 = bf16[32,2,16,128]{3,0,1,2:T(8,128)(2,1)} fusion(bf16[32,2,16,128]{3,0,1,2:T(8,128)(2,1)S(1)} %get-tuple-element.11, bf16[32,2,16,1]{3,0,1,2:T(8,128)(2,1)S(1)} %copy.60, bf16[32,2,16,1]{3,0,1,2:T(8,128)(2,1)S(1)} %copy.58, bf16[32,2,16,128]{3,2,1,0:T(8,128)(2,1)S(1)} %get-tuple-element.23, bf16[32,2,16,128]{3,2,1,0:T(8,128)(2,1)S(1)} %get-tuple-element.22, ...), kind=kLoop, calls=%fused_computation.11 | loop fusion | flops 2883584 | bytes 1314816 | tf_op jit(solution)/shard_map/convert_element_type | solution.py:41
  14.1 3.7 %all-to-all-start = ((bf16[32,2,16,128]{3,0,1,2:T(8,128)(2,1)}), bf16[32,2,16,128]{3,0,1,2:T(8,128)(2,1)S(1)}, u32[]{:S(2)}, u32[]{:S(2)}) async-start(bf16[32,2,16,128]{3,0,1,2:T(8,128)(2,1)} %fusion.4), calls=%async_computation | async-start | bytes 524288 | tf_op jit(solution)/shard_map/all_to_all | solution.py:118
  17.8 0.7 %copy-done.4 = f32[1,256]{1,0:T(1,128)S(1)} copy-done((f32[1,256]{1,0:T(1,128)S(1)}, f32[1,256]{1,0:T(1,128)}, u32[]{:S(2)}) %copy-start.4) | copy-done | bytes 1048
  18.5 0.6 %gather_fusion = f32[4]{0:T(128)S(1)} fusion(f32[4]{0:T(128)S(1)} %multiply_bitcast_fusion, s32[1024]{0:T(1024)S(1)} %pad_clamp_fusion), kind=kCustom, calls=%fused_computation.2 | custom fusion | bytes 48 | tf_op jit(solution)/shard_map/gather | solution.py:62
  19.1 5.6 %all-to-all-done = bf16[32,2,16,128]{3,0,1,2:T(8,128)(2,1)S(1)} async-done(((bf16[32,2,16,128]{3,0,1,2:T(8,128)(2,1)}), bf16[32,2,16,128]{3,0,1,2:T(8,128)(2,1)S(1)}, u32[]{:S(2)}, u32[]{:S(2)}) %all-to-all-start) | async-done | bytes 262176 | tf_op jit(solution)/shard_map/all_to_all | solution.py:118
  24.7 0.4 fusion.34
  25.1 0.3 fusion.17
  25.5 0.2 fusion.33
  25.8 1.2 %gather_fusion.1 = bf16[256,256]{1,0:T(8,128)(2,1)S(1)} fusion(bf16[256,256]{0,1:T(8,128)(2,1)S(1)} %bitcast.38, s32[1024]{0:T(1024)S(1)} %pad_clamp_fusion.1), kind=kCustom, calls=%fused_computation.clone | custom fusion | bytes 263168 | tf_op jit(solution)/shard_map/jit(_take)/gather | solution.py:48
  27.1 1.2 %gather_fusion.2 = bf16[256,256]{1,0:T(8,128)(2,1)S(1)} fusion(bf16[256,256]{0,1:T(8,128)(2,1)S(1)} %bitcast.37, s32[1024]{0:T(1024)S(1)} %pad_clamp_fusion.1), kind=kCustom, calls=%fused_computation.1.clone | custom fusion | bytes 263168 | tf_op jit(solution)/shard_map/jit(_take)/gather | solution.py:48
  28.6 0.7 %copy-done.3 = f32[1,256]{1,0:T(1,128)S(1)} copy-done((f32[1,256]{1,0:T(1,128)S(1)}, f32[1,256]{1,0:T(1,128)}, u32[]{:S(2)}) %copy-start.3) | copy-done | bytes 1048
  29.4 3.8 %collective-permute-start.3 = (bf16[258,128]{1,0:T(8,128)(2,1)S(1)}, bf16[258,128]{1,0:T(8,128)(2,1)S(1)}, u32[]{:S(2)}, u32[]{:S(2)}) collective-permute-start(bf16[258,128]{1,0:T(8,128)(2,1)S(1)} %get-tuple-element.19), channel_id=1, source_target_pairs={{1,0},{2,1},{3,2},{0,3},{5,4},{6,5},{7,6},{4,7},{9,8},{10,9},{11,1... | collective-permute-start | bytes 198152 | tf_op jit(solution)/shard_map/ppermute | solution.py:20
  33.2 0.4 reshape.45
  33.6 1.8 %collective-permute-done.2 = bf16[258,128]{1,0:T(8,128)(2,1)S(1)} collective-permute-done((bf16[258,128]{1,0:T(8,128)(2,1)S(1)}, bf16[258,128]{1,0:T(8,128)(2,1)S(1)}, u32[]{:S(2)}, u32[]{:S(2)}) %collective-permute-start.2) | collective-permute-done | bytes 66080 | tf_op jit(solution)/shard_map/ppermute | solution.py:18
  35.6 0.3 fusion.9
  35.8 0.3 abs_reduce_fusion
  36.1 0.6 %reduce_max.9 = f32[]{:T(128)} reduce(f32[256]{0:T(256)S(1)} %get-tuple-element.20, f32[]{:T(128)} %constant.48.clone.1), dimensions={0}, to_apply=%region_3.5 | reduce | flops 255 | bytes 1032 | tf_op jit(solution)/shard_map/reduce_max | solution.py:86
  37.9 0.2 convolution_bitcast_fusion
  38.1 0.3 fusion.39
  38.3 0.4 fusion
  38.8 9.3 %all_to_all.36 = bf16[256,2,2,128]{3,2,1,0:T(2,128)(2,1)S(1)} all-to-all(bf16[256,2,2,128]{3,2,1,0:T(2,128)(2,1)S(1)} %reshape.42), channel_id=1, replica_groups=mesh['member'=8,'domain'=4] {'member'}, dimensions={0} | all-to-all | bytes 524288 | tf_op jit(solution)/shard_map/all_to_all | solution.py:128
  48.1 0.9 %copy.70 = bf16[8,32,2,2,128]{4,3,0,2,1:T(2,128)(2,1)} copy(bf16[8,32,2,2,128]{4,3,2,1,0:T(2,128)(2,1)S(1)} %bitcast.41) | data formatting | bytes 524288 | tf_op jit(solution)/shard_map/all_to_all | solution.py:128
  (44 shorter events, 1.6 us)
Async XLA Ops:
  1.2 5.9 %copy-start = (bf16[32,2,16,128]{3,2,1,0:T(8,128)(2,1)S(1)}, bf16[32,2,16,128]{3,2,1,0:T(8,128)(2,1)}, u32[]{:S(2)}) copy-start(bf16[32,2,16,128]{3,2,1,0:T(8,128)(2,1)} %param.10) | copy-start | bytes 786436
  1.6 7.4 %collective-permute-start = (bf16[32,2,16,1]{0,2,3,1:T(8,128)(2,1)S(1)}, bf16[32,2,16,1]{0,2,3,1:T(8,128)(2,1)S(1)}, u32[]{:S(2)}, u32[]{:S(2)}) collective-permute-start(bf16[32,2,16,1]{0,2,3,1:T(8,128)(2,1)S(1)} %copy.71), channel_id=1, source_target_pairs={{1,0},{2,1},{3,2},{0,3},{5,4},{6,5},{7,6},{4,7},{9,8},{10,9},{11,1... | collective-permute-start | bytes 6152 | tf_op jit(solution)/shard_map/ppermute | solution.py:20
  7.1 5.5 %collective-permute-start.1 = (bf16[32,2,16,1]{0,2,3,1:T(8,128)(2,1)S(1)}, bf16[32,2,16,1]{0,2,3,1:T(8,128)(2,1)S(1)}, u32[]{:S(2)}, u32[]{:S(2)}) collective-permute-start(bf16[32,2,16,1]{0,2,3,1:T(8,128)(2,1)S(1)} %copy.72), channel_id=1, source_target_pairs={{0,1},{1,2},{2,3},{3,0},{4,5},{5,6},{6,7},{7,4},{8,9},{9,10},{10,1... | collective-permute-start | bytes 6152 | tf_op jit(solution)/shard_map/ppermute | solution.py:18
  7.4 0.7 %copy-start.1 = (s32[1,256]{1,0:T(1,128)S(1)}, s32[1,256]{1,0:T(1,128)}, u32[]{:S(2)}) copy-start(s32[1,256]{1,0:T(1,128)} %param.14) | copy-start | bytes 3076
  7.4 0.7 %copy-start.2 = (s32[1,256]{1,0:T(1,128)S(1)}, s32[1,256]{1,0:T(1,128)}, u32[]{:S(2)}) copy-start(s32[1,256]{1,0:T(1,128)} %param.13) | copy-start | bytes 3076
  8.1 0.7 %copy-start.5 = (s32[1,4]{1,0:T(1,128)S(1)}, s32[1,4]{1,0:T(1,128)}, u32[]{:S(2)}) copy-start(s32[1,4]{1,0:T(1,128)} %param.15) | copy-start | bytes 52
  8.1 0.7 %copy-start.6 = (f32[1,4]{1,0:T(1,128)S(1)}, f32[1,4]{1,0:T(1,128)}, u32[]{:S(2)}) copy-start(f32[1,4]{1,0:T(1,128)} %constant.57) | copy-start | bytes 52
  14.1 10.6 %all-to-all-start = ((bf16[32,2,16,128]{3,0,1,2:T(8,128)(2,1)}), bf16[32,2,16,128]{3,0,1,2:T(8,128)(2,1)S(1)}, u32[]{:S(2)}, u32[]{:S(2)}) async-start(bf16[32,2,16,128]{3,0,1,2:T(8,128)(2,1)} %fusion.4), calls=%async_computation | async-start | bytes 524288 | tf_op jit(solution)/shard_map/all_to_all | solution.py:118
  17.8 0.7 %copy-start.4 = (f32[1,256]{1,0:T(1,128)S(1)}, f32[1,256]{1,0:T(1,128)}, u32[]{:S(2)}) copy-start(f32[1,256]{1,0:T(1,128)} %param.12) | copy-start | bytes 3076
  28.6 0.7 %copy-start.3 = (f32[1,256]{1,0:T(1,128)S(1)}, f32[1,256]{1,0:T(1,128)}, u32[]{:S(2)}) copy-start(f32[1,256]{1,0:T(1,128)} %param.11) | copy-start | bytes 3076
  29.3 6.1 %collective-permute-start.2 = (bf16[258,128]{1,0:T(8,128)(2,1)S(1)}, bf16[258,128]{1,0:T(8,128)(2,1)S(1)}, u32[]{:S(2)}, u32[]{:S(2)}) collective-permute-start(bf16[258,128]{1,0:T(8,128)(2,1)S(1)} %get-tuple-element.18), channel_id=1, source_target_pairs={{0,1},{1,2},{2,3},{3,0},{4,5},{5,6},{6,7},{7,4},{8,9},{9,10},{10,1... | collective-permute-start | bytes 198152 | tf_op jit(solution)/shard_map/ppermute | solution.py:18
  29.4 6.1 %collective-permute-start.3 = (bf16[258,128]{1,0:T(8,128)(2,1)S(1)}, bf16[258,128]{1,0:T(8,128)(2,1)S(1)}, u32[]{:S(2)}, u32[]{:S(2)}) collective-permute-start(bf16[258,128]{1,0:T(8,128)(2,1)S(1)} %get-tuple-element.19), channel_id=1, source_target_pairs={{1,0},{2,1},{3,2},{0,3},{5,4},{6,5},{7,6},{4,7},{9,8},{10,9},{11,1... | collective-permute-start | bytes 198152 | tf_op jit(solution)/shard_map/ppermute | solution.py:20
where the time goes:
time: 49.4 us; the launch traced here: 49 us
  starting transfers between devices  12.7 us (26%)
  waiting for transfers between devices  10.6 us (21%)
  local copies, waits for them, and re-layouts  10.5 us (21%)
  blocking collectives  9.32 us (19%)
  other arithmetic  3.34 us (7%)
  matrix products  1.37 us (3%)
  between operations  1.17 us (2%)
    all_to_all x1, blocking collectives, on_device(): lax.all_to_all(analysis, 'member', split_axis=0, concat_axis=2, tiled=True)  9.32 us
    ppermute x2, starting transfers between devices, padded(): lax.ppermute(head, axis, [((i + 1) % count, i) for i in range(count)])  8.92 us
    all_to_all x1, waiting for transfers between devices, on_device(): lax.all_to_all(predicted_state, 'member', split_axis=2, concat_axis=0, ti...  5.57 us
    ppermute x2, waiting for transfers between devices, padded(): lax.ppermute(tail, axis, [(i, (i + 1) % count) for i in range(count)])  5.04 us
    all_to_all x1, starting transfers between devices, on_device(): lax.all_to_all(predicted_state, 'member', split_axis=2, concat_axis=0, ti...  3.72 us
    unnamed x18, local copies, waits for them, and re-layouts  3.63 us
    gather x2, local copies, waits for them, and re-layouts, observe(): jnp.take(tracer, obs_index, axis=1).astype(jnp.float32)  1.25 us
    gather x2, local copies, waits for them, and re-layouts, observe(): jnp.take(wind_field, obs_index, axis=1).astype(jnp.float32)  1.25 us
  transfers between devices with their start and end apart: 5, of which 3 were waited for; matrix products, arithmetic and copies ran while one was open for 5% of the time, Pallas kernels for 0%

commit v1 on v0

v1 whole, which is shorter than its diff:
```python
import functools

import jax
import jax.numpy as jnp
from jax import lax
from jax.experimental import pallas as pl
from jax.experimental.pallas import tpu as pltpu
from jax.sharding import PartitionSpec as P

ADVECT = 0.4
DIFFUSE = 0.15
OBS_WIND = 0.5
TAPER = (0.5, 1.0, 1.0, 0.5)
MESH = pl.DeviceIdType.MESH
F32 = jnp.float32
BF16 = jnp.bfloat16


def remote(src, dst, send, recv, where):
    return pltpu.make_async_remote_copy(
        src_ref=src, dst_ref=dst, send_sem=send, recv_sem=recv, device_id=where, device_id_type=MESH
    )


def kernel(
    nm, nd, ens, value, prec, row, col, mask, out,
    raw, val_v, prec_v, row_v, col_v, mask_v, rows_f32, halo_out, halo_in, bands, cells, obs_own, obs_in,
    back, got, load_sem, halo_send, halo_recv, out_send, out_recv, obs_send, obs_recv, back_send, back_recv,
):
    me_m = lax.axis_index("member")
    me_d = lax.axis_index("domain")
    east = lax.rem(me_d + 1, nd)
    west = lax.rem(me_d + nd - 1, nd)
    peers = [lax.rem(me_m + i, nm) for i in range(nm)]
    froms = [lax.rem(me_m + nm - i, nm) for i in range(nm)]
    own, fields, nrows, ncols = raw.shape
    reg = nrows // nm
    members = own * nm
    pitch = fields * nrows

    barrier = pltpu.get_barrier_semaphore()
    for i in range(1, nm):
        pl.semaphore_signal(barrier, inc=1, device_id={"member": peers[i]}, device_id_type=MESH)
    for near in (east, west):
        pl.semaphore_signal(barrier, inc=1, device_id={"domain": near}, device_id_type=MESH)
    loads = [
        pltpu.make_async_copy(src, dst, load_sem.at[i])
        for i, (src, dst) in enumerate(
            [(ens, raw), (value, val_v), (prec, prec_v), (row, row_v), (col, col_v), (mask, mask_v)]
        )
    ]
    for load in loads:
        load.start()
    loads[0].wait()

    rows_f32[...] = raw[...].astype(F32).reshape(own * pitch, ncols)

    def line(f, r):
        return rows_f32[pl.ds(f * nrows + r % nrows, own, stride=pitch), :]

    lane = lax.broadcasted_iota(jnp.int32, (own, ncols), 1)
    first = jnp.zeros((own, ncols), F32)
    last = jnp.zeros((own, ncols), F32)
    for f in range(fields):
        for r in range(nrows):
            spot = f * nrows + r
            here = line(f, r)
            first = jnp.where(lane == spot, pltpu.roll(here, spot % ncols, 1), first)
            last = jnp.where(lane == spot, pltpu.roll(here, (spot + 1) % ncols, 1), last)
    halo_out[0] = first.astype(BF16)
    halo_out[1] = last.astype(BF16)
    pl.semaphore_wait(barrier, nm + 1)
    halos = [
        remote(halo_out.at[0], halo_in.at[0], halo_send.at[0], halo_recv.at[0], {"domain": west}),
        remote(halo_out.at[1], halo_in.at[1], halo_send.at[1], halo_recv.at[1], {"domain": east}),
    ]
    for copy in halos:
        copy.start()
    for load in loads[1:]:
        load.wait()
    nobs = val_v.shape[1]
    half = nobs // 2
    index = row_v[...] * ncols + col_v[...]
    spots = lax.broadcasted_iota(jnp.int32, (reg * ncols, nobs), 0)
    hit = jnp.where(spots == index, 1.0, 0.0)
    pick = jnp.concatenate([(OBS_WIND * hit).astype(BF16), hit.astype(BF16)], axis=0)
    for copy in halos:
        copy.wait_recv()

    from_east = halo_in[0].astype(F32)
    from_west = halo_in[1].astype(F32)

    def forecast(f, r):
        spot = f * nrows + r
        middle = line(f, r)
        shape = middle.shape
        east_side = jnp.where(
            lane == ncols - 1,
            jnp.broadcast_to(from_east[:, spot : spot + 1], shape),
            pltpu.roll(middle, ncols - 1, 1),
        )
        west_side = jnp.where(
            lane == 0, jnp.broadcast_to(from_west[:, spot : spot + 1], shape), pltpu.roll(middle, 1, 1)
        )
        laplace = east_side + west_side + line(f, r + 1) + line(f, r - 1) - 4.0 * middle
        return (
            middle - ADVECT * 0.5 * line(0, r) * (east_side - west_side) + DIFFUSE * laplace
        ).astype(BF16)

    for m in range(nm):
        for f in range(fields):
            for r in range(reg):
                bands[m, f * reg + r] = forecast(f, m * reg + r)

    def mine(block):
        return pl.ds(pl.multiple_of(block * own, own), own)

    sends = []
    for i in range(1, nm):
        copy = remote(
            bands.at[peers[i]], cells.at[:, mine(me_m), :], out_send.at[i], out_recv.at[i], {"member": peers[i]}
        )
        copy.start()
        sends.append(copy)
    cells[:, mine(me_m), :] = bands[me_m]
    for i in range(1, nm):
        remote(
            bands.at[froms[i]], cells.at[:, mine(froms[i]), :], out_send.at[i], out_recv.at[i], {"member": froms[i]}
        ).wait_recv()

    count = fields * reg
    state = jnp.concatenate([cells[i] for i in range(count)], axis=1)
    equivalent = jnp.dot(state, pick, preferred_element_type=F32)
    center = jnp.sum(equivalent, axis=0, keepdims=True) * (1.0 / members)
    scaled = ((equivalent - center) * (members - 1) ** (-0.5)).astype(BF16)
    tail_row = lax.broadcasted_iota(jnp.int32, (16, nobs), 0)
    tail = jnp.where(
        tail_row == 0, val_v[...] - center, jnp.where(tail_row == 1, prec_v[...], 0.0)
    ).astype(BF16)
    for side in range(2):
        part = slice(side * half, (side + 1) * half)
        obs_own[side, 0:members] = scaled[:, part]
        obs_own[side, members : members + 16] = tail[:, part]
    swaps = [
        remote(obs_own.at[0], obs_in.at[1], obs_send.at[0], obs_recv.at[1], {"domain": west}),
        remote(obs_own.at[1], obs_in.at[0], obs_send.at[1], obs_recv.at[0], {"domain": east}),
    ]
    for copy in swaps:
        copy.start()

    wide = state.astype(F32)
    ens_mean = jnp.sum(wide, axis=0, keepdims=True) * (1.0 / members)
    anomalies = (wide - ens_mean).astype(BF16)

    def term(block, which):
        rows = block[0:members]
        ends = block[members : members + 16]
        use = TAPER[which] * mask_v[0:1, which : which + 1].astype(F32)
        weight = ends[1:2].astype(F32) * use
        weighted = (rows.astype(F32) * weight).astype(BF16)
        part = lax.dot_general(rows, weighted, (((1,), (1,)), ((), ())), preferred_element_type=F32)
        push = lax.dot_general(weighted, ends, (((1,), (1,)), ((), ())), preferred_element_type=F32)
        return part, push[:, 0:1]

    cross, forcing = term(obs_own[0], 1)
    more, push = term(obs_own[1], 2)
    cross, forcing = cross + more, forcing + push
    swaps[1].wait_recv()
    more, push = term(obs_in[0], 0)
    cross, forcing = cross + more, forcing + push
    swaps[0].wait_recv()
    more, push = term(obs_in[1], 3)
    cross, forcing = cross + more, forcing + push

    cross_half = cross.astype(BF16)
    squared = jnp.dot(cross_half, cross_half, preferred_element_type=F32)
    sums = jnp.sum(jnp.abs(squared), axis=0, keepdims=True)
    bound = jnp.sqrt(jnp.max(sums, axis=1, keepdims=True))
    delta = (bound + 1.0) / 2.0
    theta = 1.0 + delta
    sigma = theta / delta
    rho0 = 1.0 / sigma
    rho1 = 1.0 / (2.0 * sigma - rho0)
    rest = 1.0 - 1.0 / theta
    keep = 1.0 + rho1 * rho0
    on_eye = 1.0 / theta + keep * rest / theta + 2.0 * rho1 / delta * rest * rest
    on_cross = -(keep + 4.0 * rho1) / (theta * theta)
    on_square = 2.0 * rho1 / (delta * theta * theta)
    eye = lax.broadcasted_iota(jnp.int32, (members, members), 0) == lax.broadcasted_iota(
        jnp.int32, (members, members), 1
    )
    inverse = jnp.where(eye, on_eye, 0.0) + on_cross * cross + on_square * squared
    mean_weights = jnp.sum(inverse * forcing, axis=0, keepdims=True)
    transform = (
        0.5 * (jnp.where(eye, 1.0, 0.0) + inverse) + mean_weights * (members - 1) ** (-0.5)
    ).astype(BF16)
    analysis = (
        ens_mean + jnp.dot(transform, anomalies, preferred_element_type=F32)
    ).astype(BF16)
    for i in range(count):
        back[i] = analysis[:, i * ncols : (i + 1) * ncols]
    returns = []
    for i in range(1, nm):
        copy = remote(
            back.at[:, mine(peers[i]), :], got.at[me_m], back_send.at[i], back_recv.at[i], {"member": peers[i]}
        )
        copy.start()
        returns.append(copy)
    got[me_m] = back[:, mine(me_m), :]
    for i in range(1, nm):
        remote(
            back.at[:, mine(froms[i]), :], got.at[froms[i]], back_send.at[i], back_recv.at[i], {"member": froms[i]}
        ).wait_recv()
    for m in range(nm):
        for f in range(fields):
            for r in range(reg):
                rows_f32[pl.ds(f * nrows + m * reg + r, own, stride=pitch), :] = got[m, f * reg + r].astype(F32)
    out[...] = rows_f32[...].reshape(own, fields, nrows, ncols).astype(BF16)
    for copy in halos + sends + swaps + returns:
        copy.wait_send()


def solution(mesh):
    nm, nd = mesh.shape["member"], mesh.shape["domain"]

    def on_device(ensemble, obs_value, obs_prec, obs_row, obs_col, loc_mask):
        own, fields, nrows, ncols = ensemble.shape
        reg = nrows // nm
        members = own * nm
        nobs = obs_value.shape[1]
        vm = pltpu.VMEM
        dma = pltpu.SemaphoreType.DMA
        return pl.pallas_call(
            functools.partial(kernel, nm, nd),
            out_shape=jax.ShapeDtypeStruct(ensemble.shape, BF16),
            in_specs=[pl.BlockSpec(memory_space=pl.ANY)] * 6,
            out_specs=pl.BlockSpec(memory_space=pltpu.VMEM),
            scratch_shapes=[
                vm(ensemble.shape, BF16),
                vm((1, nobs), F32),
                vm((1, nobs), F32),
                vm((1, nobs), jnp.int32),
                vm((1, nobs), jnp.int32),
                vm(loc_mask.shape, jnp.int32),
                vm((own * fields * nrows, ncols), F32),
                vm((2, own, ncols), BF16),
                vm((2, own, ncols), BF16),
                vm((nm, fields * reg, own, ncols), BF16),
                vm((fields * reg, members, ncols), BF16),
                vm((2, members + 16, nobs // 2), BF16),
                vm((2, members + 16, nobs // 2), BF16),
                vm((fields * reg, members, ncols), BF16),
                vm((nm, fields * reg, own, ncols), BF16),
                dma((6,)),
                dma((2,)),
                dma((2,)),
                dma((nm,)),
                dma((nm,)),
                dma((2,)),
                dma((2,)),
                dma((nm,)),
                dma((nm,)),
            ],
            compiler_params=pltpu.CompilerParams(collective_id=0, has_side_effects=True),
        )(ensemble, obs_value, obs_prec, obs_row, obs_col, loc_mask)

    in_specs = (P("member", None, None, "domain"),) + (P("member", "domain"),) * 5
    return jax.shard_map(
        on_device, mesh=mesh, in_specs=in_specs, out_specs=P("member", None, None, "domain"), check_vma=False
    )
```

time: 49.4 us -> 29 us (0.59)
  Pallas kernels: 0 us -> 27.1 us
  starting transfers between devices: 12.7 us -> 0 us
  waiting for transfers between devices: 10.6 us -> 0 us
  blocking collectives: 9.32 us -> 0 us
  local copies, waits for them, and re-layouts: 10.5 us -> 1.67 us
  other arithmetic: 3.34 us -> 0 us
  matrix products: 1.37 us -> 0 us
  between operations: 1.17 us -> 0.01 us
    pallas_call x0 -> x1, Pallas kernels: none -> 27.1 us  [on_device(): pl.pallas_call(functools.partial(kernel, nm, nd), out_shape=jax.ShapeDtyp...]
    all_to_all x1 -> x0, blocking collectives: 9.32 us -> none  [on_device(): lax.all_to_all(analysis, 'member', split_axis=0, concat_axis=2, tiled=True)]
    ppermute x4 -> x0, starting transfers between devices: 9.01 us -> none  [the longest x2 8.92 us: padded(): lax.ppermute(head, axis, [((i + 1) % count, i) for i in range(count)])]
    all_to_all x1 -> x0, waiting for transfers between devices: 5.57 us -> none  [on_device(): lax.all_to_all(predicted_state, 'member', split_axis=2, concat_axis=0, ti...]
    ppermute x4 -> x0, waiting for transfers between devices: 5.05 us -> none  [the longest x2 5.04 us: padded(): lax.ppermute(tail, axis, [(i, (i + 1) % count) for i in range(count)])]
    all_to_all x1 -> x0, starting transfers between devices: 3.72 us -> none  [on_device(): lax.all_to_all(predicted_state, 'member', split_axis=2, concat_axis=0, ti...]
    gather x5 -> x0, local copies, waits for them, and re-layouts: 3.14 us -> none  [the longest x2 1.25 us: observe(): jnp.take(tracer, obs_index, axis=1).astype(jnp.float32)]
    unnamed x18 -> x1, local copies, waits for them, and re-layouts: 3.63 us -> 1.67 us
  transfers between devices with their start and end apart: 5 -> 0, of which waited for: 3 -> 0; matrix products, arithmetic and copies ran while one was open for 5% -> 0% of each run, Pallas kernels for 0% -> 0%
where the time goes in v1:
time: 29 us; the launch traced here: 28.8 us
  Pallas kernels  27.1 us (93%)
  local copies, waits for them, and re-layouts  1.67 us (6%)
    pallas_call x1, Pallas kernels, on_device(): pl.pallas_call(functools.partial(kernel, nm, nd), out_shape=jax.ShapeDtyp...  27.1 us
    unnamed x1, local copies, waits for them, and re-layouts  1.67 us

profile of v1, /device:TPU:0, one launch (start us, length us, event | category | flops | bytes accessed | tf_op | source)
XLA Modules:
  0.0 28.8 jit_solution(6024435358603234560)
XLA Ops:
  0.0 27.1 %shard_map.64 = bf16[32,2,16,128]{3,2,1,0:T(8,128)(2,1)} custom-call(bf16[32,2,16,128]{3,2,1,0:T(8,128)(2,1)} %ens.1, f32[1,256]{1,0:T(1,128)} %value.1, f32[1,256]{1,0:T(1,128)} %prec.1, s32[1,256]{1,0:T(1,128)} %row.1, s32[1,256]{1,0:T(1,128)} %col.1, s32[1,4]{1,0:T(1,128)} %mask.1), custom_call_target="tpu_custom_call" | custom-call | tf_op jit(solution)/shard_map/pallas_call | solution.py:233
  27.1 1.7 %copy.8 = bf16[32,2,16,128]{3,2,1,0:T(8,128)(2,1)} copy(bf16[32,2,16,128]{3,2,1,0:T(8,128)(2,1)} %shard_map.64) | data formatting | bytes 524288

commit v2 on v1

--- a/solution.py
+++ b/solution.py
@@ -23,9 +23,9 @@
 
 
 def kernel(
-    nm, nd, ens, value, prec, row, col, mask, out,
-    raw, val_v, prec_v, row_v, col_v, mask_v, rows_f32, halo_out, halo_in, bands, cells, obs_own, obs_in,
-    back, got, load_sem, halo_send, halo_recv, out_send, out_recv, obs_send, obs_recv, back_send, back_recv,
+    nm, nd, ens, value, prec, row, col, mask, got,
+    raw, val_v, prec_v, row_v, col_v, mask_v, rows_f32, halo_out, halo_in, bands, cells, edge_out, edge_in, obs_own, obs_in,
+    back, load_sem, halo_send, halo_recv, out_send, out_recv, edge_send, edge_recv, obs_send, obs_recv, back_send, back_recv,
 ):
     me_m = lax.axis_index("member")
     me_d = lax.axis_index("domain")
@@ -56,17 +56,21 @@
     rows_f32[...] = raw[...].astype(F32).reshape(own * pitch, ncols)
 
     def line(f, r):
-        return rows_f32[pl.ds(f * nrows + r % nrows, own, stride=pitch), :]
+        return rows_f32[pl.ds(f * nrows + (r % nrows if isinstance(r, int) else lax.rem(r, nrows)), own, stride=pitch), :]
 
     lane = lax.broadcasted_iota(jnp.int32, (own, ncols), 1)
-    first = jnp.zeros((own, ncols), F32)
-    last = jnp.zeros((own, ncols), F32)
-    for f in range(fields):
-        for r in range(nrows):
-            spot = f * nrows + r
-            here = line(f, r)
-            first = jnp.where(lane == spot, pltpu.roll(here, spot % ncols, 1), first)
-            last = jnp.where(lane == spot, pltpu.roll(here, (spot + 1) % ncols, 1), last)
+    used = fields * nrows
+
+    def packed(column):
+        total = jnp.zeros((own, ncols), F32)
+        for f in range(fields):
+            for r in range(nrows):
+                spot = f * nrows + r
+                moved = pltpu.roll(line(f, r), (spot - column) % ncols, 1)
+                total = jnp.where(lane == spot, moved, total)
+        return total
+
+    first, last = packed(0), packed(ncols - 1)
     halo_out[0] = first.astype(BF16)
     halo_out[1] = last.astype(BF16)
     pl.semaphore_wait(barrier, nm + 1)
@@ -76,6 +80,76 @@
     ]
     for copy in halos:
         copy.start()
+
+    def mine(block):
+        return pl.ds(pl.multiple_of(block * own, own), own)
+
+    def step(middle, east_side, west_side, north, south, wind):
+        laplace = east_side + west_side + north + south - 4.0 * middle
+        return (middle - ADVECT * 0.5 * wind * (east_side - west_side) + DIFFUSE * laplace).astype(BF16)
+
+    def interior(m, f, r):
+        at = m * reg + r
+        middle = line(f, at)
+        return step(
+            middle, pltpu.roll(middle, ncols - 1, 1), pltpu.roll(middle, 1, 1),
+            line(f, at + 1), line(f, at + nrows - 1), line(0, at),
+        )
+
+    sends = []
+    for i in list(range(1, nm)) + [0]:
+        m = peers[i]
+        for f in range(fields):
+            for r in range(reg):
+                if i:
+                    bands[i, f * reg + r] = interior(m, f, r)
+                else:
+                    cells[f * reg + r, mine(me_m), :] = interior(m, f, r)
+        if i:
+            copy = remote(bands.at[i], cells.at[:, mine(me_m), :], out_send.at[i], out_recv.at[i], {"member": m})
+            copy.start()
+            sends.append(copy)
+
+    second, prior = packed(1), packed(ncols - 2)
+    row_of = lax.rem(lane, nrows)
+
+    def north_of(x):
+        return jnp.where(row_of == nrows - 1, pltpu.roll(x, nrows - 1, 1), pltpu.roll(x, ncols - 1, 1))
+
+    def south_of(x):
+        return jnp.where(row_of == 0, pltpu.roll(x, ncols - nrows + 1, 1), pltpu.roll(x, 1, 1))
+
+    def wind_of(x):
+        total = x
+        for f in range(1, fields):
+            total = jnp.where(lane // nrows == f, pltpu.roll(x, f * nrows, 1), total)
+        return total
+
+    for copy in halos:
+        copy.wait_recv()
+    edge_first = step(
+        first, second, halo_in[1].astype(F32), north_of(first), south_of(first), wind_of(first)
+    )
+    edge_last = step(
+        last, halo_in[0].astype(F32), prior, north_of(last), south_of(last), wind_of(last)
+    )
+    layers = edge_out.shape[0]
+    if layers == 1:
+        edge_out[0] = jnp.where(
+            lane < used, edge_first.astype(F32), pltpu.roll(edge_last.astype(F32), used, 1)
+        ).astype(BF16)
+    else:
+        edge_out[0] = edge_first
+        edge_out[1] = edge_last
+    for i in range(1, nm):
+        copy = remote(
+            edge_out, edge_in.at[:, mine(me_m), :], edge_send.at[i], edge_recv.at[i], {"member": peers[i]}
+        )
+        copy.start()
+        sends.append(copy)
+    for k in range(layers):
+        edge_in[k, mine(me_m), :] = edge_out[k]
+
     for load in loads[1:]:
         load.wait()
     nobs = val_v.shape[1]
@@ -84,52 +158,34 @@
     spots = lax.broadcasted_iota(jnp.int32, (reg * ncols, nobs), 0)
     hit = jnp.where(spots == index, 1.0, 0.0)
     pick = jnp.concatenate([(OBS_WIND * hit).astype(BF16), hit.astype(BF16)], axis=0)
-    for copy in halos:
-        copy.wait_recv()
-
-    from_east = halo_in[0].astype(F32)
-    from_west = halo_in[1].astype(F32)
-
-    def forecast(f, r):
+
+    for i in range(1, nm):
+        remote(
+            bands.at[i], cells.at[:, mine(froms[i]), :], out_send.at[i], out_recv.at[i], {"member": froms[i]}
+        ).wait_recv()
+    for i in range(1, nm):
+        remote(
+            edge_out, edge_in.at[:, mine(froms[i]), :], edge_send.at[i], edge_recv.at[i], {"member": froms[i]}
+        ).wait_recv()
+    lead = lax.rem(ncols - me_m * reg, ncols)
+    edges = [pltpu.roll(edge_in[k].astype(F32), lead, 1) for k in range(layers)]
+    wide_lane = lax.broadcasted_iota(jnp.int32, (members, ncols), 1)
+
+    def whole(f, r):
         spot = f * nrows + r
-        middle = line(f, r)
-        shape = middle.shape
-        east_side = jnp.where(
-            lane == ncols - 1,
-            jnp.broadcast_to(from_east[:, spot : spot + 1], shape),
-            pltpu.roll(middle, ncols - 1, 1),
-        )
-        west_side = jnp.where(
-            lane == 0, jnp.broadcast_to(from_west[:, spot : spot + 1], shape), pltpu.roll(middle, 1, 1)
-        )
-        laplace = east_side + west_side + line(f, r + 1) + line(f, r - 1) - 4.0 * middle
-        return (
-            middle - ADVECT * 0.5 * line(0, r) * (east_side - west_side) + DIFFUSE * laplace
-        ).astype(BF16)
-
-    for m in range(nm):
-        for f in range(fields):
-            for r in range(reg):
-                bands[m, f * reg + r] = forecast(f, m * reg + r)
-
-    def mine(block):
-        return pl.ds(pl.multiple_of(block * own, own), own)
-
-    sends = []
-    for i in range(1, nm):
-        copy = remote(
-            bands.at[peers[i]], cells.at[:, mine(me_m), :], out_send.at[i], out_recv.at[i], {"member": peers[i]}
-        )
-        copy.start()
-        sends.append(copy)
-    cells[:, mine(me_m), :] = bands[me_m]
-    for i in range(1, nm):
-        remote(
-            bands.at[froms[i]], cells.at[:, mine(froms[i]), :], out_send.at[i], out_recv.at[i], {"member": froms[i]}
-        ).wait_recv()
+        left = edges[0][:, spot : spot + 1]
+        if layers == 1:
+            right = edges[0][:, used + spot : used + spot + 1]
+        else:
+            right = edges[1][:, spot : spot + 1]
+        shape = (members, ncols)
+        inner = cells[f * reg + r].astype(F32)
+        inner = jnp.where(wide_lane == 0, jnp.broadcast_to(left, shape), inner)
+        return jnp.where(wide_lane == ncols - 1, jnp.broadcast_to(right, shape), inner)
 
     count = fields * reg
-    state = jnp.concatenate([cells[i] for i in range(count)], axis=1)
+    wide = jnp.concatenate([whole(f, r) for f in range(fields) for r in range(reg)], axis=1)
+    state = wide.astype(BF16)
     equivalent = jnp.dot(state, pick, preferred_element_type=F32)
     center = jnp.sum(equivalent, axis=0, keepdims=True) * (1.0 / members)
     scaled = ((equivalent - center) * (members - 1) ** (-0.5)).astype(BF16)
@@ -148,7 +204,6 @@
     for copy in swaps:
         copy.start()
 
-    wide = state.astype(F32)
     ens_mean = jnp.sum(wide, axis=0, keepdims=True) * (1.0 / members)
     anomalies = (wide - ens_mean).astype(BF16)
 
@@ -211,11 +266,6 @@
         remote(
             back.at[:, mine(froms[i]), :], got.at[froms[i]], back_send.at[i], back_recv.at[i], {"member": froms[i]}
         ).wait_recv()
-    for m in range(nm):
-        for f in range(fields):
-            for r in range(reg):
-                rows_f32[pl.ds(f * nrows + m * reg + r, own, stride=pitch), :] = got[m, f * reg + r].astype(F32)
-    out[...] = rows_f32[...].reshape(own, fields, nrows, ncols).astype(BF16)
     for copy in halos + sends + swaps + returns:
         copy.wait_send()
 
@@ -228,11 +278,13 @@
         reg = nrows // nm
         members = own * nm
         nobs = obs_value.shape[1]
+        layers = pl.cdiv(2 * fields * nrows, ncols)
+        grant = 8 * 1024 * 1024 + 32 * members * members
         vm = pltpu.VMEM
         dma = pltpu.SemaphoreType.DMA
-        return pl.pallas_call(
+        parts = pl.pallas_call(
             functools.partial(kernel, nm, nd),
-            out_shape=jax.ShapeDtypeStruct(ensemble.shape, BF16),
+            out_shape=jax.ShapeDtypeStruct((nm, fields * reg, own, ncols), BF16),
             in_specs=[pl.BlockSpec(memory_space=pl.ANY)] * 6,
             out_specs=pl.BlockSpec(memory_space=pltpu.VMEM),
             scratch_shapes=[
@@ -247,22 +299,27 @@
                 vm((2, own, ncols), BF16),
                 vm((nm, fields * reg, own, ncols), BF16),
                 vm((fields * reg, members, ncols), BF16),
+                vm((layers, own, ncols), BF16),
+                vm((layers, members, ncols), BF16),
                 vm((2, members + 16, nobs // 2), BF16),
                 vm((2, members + 16, nobs // 2), BF16),
                 vm((fields * reg, members, ncols), BF16),
-                vm((nm, fields * reg, own, ncols), BF16),
                 dma((6,)),
                 dma((2,)),
                 dma((2,)),
                 dma((nm,)),
                 dma((nm,)),
+                dma((nm,)),
+                dma((nm,)),
                 dma((2,)),
                 dma((2,)),
                 dma((nm,)),
                 dma((nm,)),
             ],
-            compiler_params=pltpu.CompilerParams(collective_id=0, has_side_effects=True),
-        )(ensemble, obs_value, obs_prec, obs_row, obs_col, loc_mask)
+            compiler_params=pltpu.CompilerParams(collective_id=0, has_side_effects=True, vmem_limit_bytes=grant),
+        )(*(pltpu.with_memory_space_constraint(x, pltpu.HBM) for x in (ensemble, obs_value, obs_prec, obs_row, obs_col, loc_mask)))
+        parts = parts.reshape(nm, fields, reg, own, ncols)
+        return jnp.transpose(parts, (3, 1, 0, 2, 4)).reshape(ensemble.shape)
 
     in_specs = (P("member", None, None, "domain"),) + (P("member", "domain"),) * 5
     return jax.shard_map(

time: 29 us -> 25.5 us (0.88)
  Pallas kernels: 27.1 us -> 24.5 us
  local copies, waits for them, and re-layouts: 1.67 us -> 0.91 us
    pallas_call x1, Pallas kernels: 27.1 us -> 24.5 us  [on_device(): pl.pallas_call(functools.partial(kernel, nm, nd), out_shape=jax.ShapeDtyp...]
    unnamed x1 -> x0, local copies, waits for them, and re-layouts: 1.67 us -> none
    transpose x0 -> x1, local copies, waits for them, and re-layouts: none -> 0.91 us  [on_device(): return jnp.transpose(parts, (3, 1, 0, 2, 4)).reshape(ensemble.shape)]
where the time goes in v2:
time: 25.5 us; the launch traced here: 25.4 us
  Pallas kernels  24.5 us (96%)
  local copies, waits for them, and re-layouts  0.91 us (4%)
    pallas_call x1, Pallas kernels, on_device(): pl.pallas_call(functools.partial(kernel, nm, nd), out_shape=jax.ShapeDtyp...  24.5 us
    transpose x1, local copies, waits for them, and re-layouts, on_device(): return jnp.transpose(parts, (3, 1, 0, 2, 4)).reshape(ensemble.shape)  0.91 us

profile of v2, /device:TPU:0, one launch (start us, length us, event | category | flops | bytes accessed | tf_op | source)
XLA Modules:
  0.0 25.4 jit_solution(17055625418578366798)
XLA Ops:
  0.0 24.5 %shard_map.64 = bf16[8,4,32,128]{3,2,1,0:T(8,128)(2,1)S(1)} custom-call(bf16[32,2,16,128]{3,2,1,0:T(8,128)(2,1)} %ens.1, f32[1,256]{1,0:T(1,128)} %value.1, f32[1,256]{1,0:T(1,128)} %prec.1, s32[1,256]{1,0:T(1,128)} %row.1, s32[1,256]{1,0:T(1,128)} %col.1, s32[1,4]{1,0:T(1,128)} %mask.1), custom_call_target="tpu_custom_call" | custom-call | tf_op jit(solution)/shard_map/pallas_call | solution.py:285
  24.5 0.9 %copy.7 = bf16[32,2,8,2,128]{4,3,2,1,0:T(2,128)(2,1)} copy(bf16[32,2,8,2,128]{4,0,3,1,2:T(8,128)(2,1)S(1)} %bitcast.4) | data formatting | bytes 524288 | tf_op jit(solution)/shard_map/transpose | solution.py:322

commit v3 on v2

--- a/solution.py
+++ b/solution.py
@@ -207,24 +207,27 @@
     ens_mean = jnp.sum(wide, axis=0, keepdims=True) * (1.0 / members)
     anomalies = (wide - ens_mean).astype(BF16)
 
-    def term(block, which):
+    def term(blocks, whichs):
+        block = jnp.concatenate(blocks, axis=1)
         rows = block[0:members]
         ends = block[members : members + 16]
-        use = TAPER[which] * mask_v[0:1, which : which + 1].astype(F32)
+        use = jnp.concatenate(
+            [
+                jnp.broadcast_to(TAPER[which] * mask_v[0:1, which : which + 1].astype(F32), (1, half))
+                for which in whichs
+            ],
+            axis=1,
+        )
         weight = ends[1:2].astype(F32) * use
         weighted = (rows.astype(F32) * weight).astype(BF16)
         part = lax.dot_general(rows, weighted, (((1,), (1,)), ((), ())), preferred_element_type=F32)
         push = lax.dot_general(weighted, ends, (((1,), (1,)), ((), ())), preferred_element_type=F32)
         return part, push[:, 0:1]
 
-    cross, forcing = term(obs_own[0], 1)
-    more, push = term(obs_own[1], 2)
-    cross, forcing = cross + more, forcing + push
+    cross, forcing = term([obs_own[0], obs_own[1]], (1, 2))
     swaps[1].wait_recv()
-    more, push = term(obs_in[0], 0)
-    cross, forcing = cross + more, forcing + push
     swaps[0].wait_recv()
-    more, push = term(obs_in[1], 3)
+    more, push = term([obs_in[0], obs_in[1]], (0, 3))
     cross, forcing = cross + more, forcing + push
 
     cross_half = cross.astype(BF16)

time: 25.5 us -> 25.5 us (level)
  no operation moved by 1% of the time
where the time goes in v3:
time: 25.5 us; the launch traced here: 25.3 us
  Pallas kernels  24.4 us (96%)
  local copies, waits for them, and re-layouts  0.91 us (4%)
    pallas_call x1, Pallas kernels, on_device(): pl.pallas_call(functools.partial(kernel, nm, nd), out_shape=jax.ShapeDtyp...  24.4 us
    transpose x1, local copies, waits for them, and re-layouts, on_device(): return jnp.transpose(parts, (3, 1, 0, 2, 4)).reshape(ensemble.shape)  0.91 us

profile of v3, /device:TPU:0, one launch (start us, length us, event | category | flops | bytes accessed | tf_op | source)
XLA Modules:
  0.0 25.3 jit_solution(845721812904179967)
XLA Ops:
  0.0 24.4 %shard_map.64 = bf16[8,4,32,128]{3,2,1,0:T(8,128)(2,1)S(1)} custom-call(bf16[32,2,16,128]{3,2,1,0:T(8,128)(2,1)} %ens.1, f32[1,256]{1,0:T(1,128)} %value.1, f32[1,256]{1,0:T(1,128)} %prec.1, s32[1,256]{1,0:T(1,128)} %row.1, s32[1,256]{1,0:T(1,128)} %col.1, s32[1,4]{1,0:T(1,128)} %mask.1), custom_call_target="tpu_custom_call" | custom-call | tf_op jit(solution)/shard_map/pallas_call | solution.py:288
  24.4 0.9 %copy.7 = bf16[32,2,8,2,128]{4,3,2,1,0:T(2,128)(2,1)} copy(bf16[32,2,8,2,128]{4,0,3,1,2:T(8,128)(2,1)S(1)} %bitcast.4) | data formatting | bytes 524288 | tf_op jit(solution)/shard_map/transpose | solution.py:325
